TPU v7x, 256 devices: a whole 4x4x8 slice. The times are simulated.
256 devices in a mesh: occ: 32 (over x, z_lo, core), aux: 8 (over y, z_hi).
Axes of the slice: x: 4, y: 4, z: 8 (z_hi: 2, z_lo: 4; z = z_hi * 4 + z_lo), core: 2. Of those that a mesh axis runs over, the one named last changes fastest.
Arguments:
- b_factors: bfloat16 [32, 256, 12288], P('occ', None, 'aux'), may hold values from -0.056884766 to 0.056884766
- occ_energies: float32 [32], P('occ'), may hold values from -1.2 to -0.3
- vir_energies: float32 [256], replicated, may hold values from 0.1 to 4
- pair_list: int32 [32, 48, 3], P('occ'), may hold values from -1 to 31, as said below
- pair_count: int32 [32], P('occ'), may hold values from 1 to 48, as said below
Outputs:
- pair_energy: float32 [32, 48], P('occ', 'aux')
- total_energy: float32 [], replicated
Inputs may be any that keep to these rules, and one draw needn't show every extreme that they name: `pair_list`: row i lists pair_count[i] distinct items (j, a-block, b-block) with j in 0 to 31 and blocks in 0 to 1, ordered by j, then a-block, then b-block; its other slots hold -1 in all three fields. `pair_count`: some occupied orbital lists exactly 48 items.
All inputs are finite; a program needn't handle non-finite values.
Results may differ from a plain program's by a relative error of at most 0.0003.
Values may be sent and summed in bfloat16 or wider, within the bound.
A program may use at most 128 MiB of HBM per device.

v0:
```python
import jax
import jax.numpy as jnp
from jax import lax
from jax.sharding import Mesh
from jax.sharding import PartitionSpec as P

VB = 128
OCC = ("occ_0", "occ_1", "occ_2")
AUX = ("aux_0", "aux_1")
OCC_AUX = ("occ_0", "occ_1", "occ_2", "aux_0", "aux_1")


def joined_along(pieces, dim):
    pieces = jnp.moveaxis(pieces, 0, dim)
    lengths = pieces.shape
    return pieces.reshape(*lengths[:dim], lengths[dim] * lengths[dim + 1], *lengths[dim + 2 :])


def sent_to_all(array, axis):
    count = lax.axis_size(axis)
    return lax.all_to_all(
        jnp.broadcast_to(array[None], (count, *array.shape)), axis, 0, 0, tiled=True
    )


def gathered_copies(array, axis, dim):
    return joined_along(sent_to_all(array, axis), dim)


def summed_rows(array, axes, dim):
    for axis in axes:
        array = lax.psum_scatter(array, axis, scatter_dimension=dim, tiled=True)
    return array


def by_axis(array, axes):
    for axis in axes:
        array = lax.psum(array, axis)
    return array


def local(b_factors, occ_energies, vir_energies, pair_list, pair_count):
    home_panel = b_factors[0]
    item_table = pair_list[0]
    slot_count = pair_count[0]
    slot_total = item_table.shape[0]
    virt_width = home_panel.shape[0]
    block_count = virt_width // VB
    live_slots = jnp.arange(slot_total, dtype=jnp.int32) < slot_count
    all_occ = gathered_copies(occ_energies, OCC, 0)
    cycle_width = lax.axis_size(OCC)
    shard_rows = b_factors.shape[0]
    orbital_total = cycle_width * shard_rows
    contract = (((1,), (2,)), ((), ()))
    block = lax.dot_general(
        home_panel,
        lax.all_gather(b_factors, OCC, axis=0, tiled=True),
        contract,
        preferred_element_type=jnp.float32,
    )
    block = jnp.transpose(block, (1, 0, 2))
    tiles = block.reshape(orbital_total, block_count, VB, block_count, VB)
    tiles = jnp.transpose(tiles, (0, 1, 3, 2, 4)).reshape(
        orbital_total * block_count * block_count, VB, VB
    )
    partner_ids = jnp.maximum(item_table[:, 0], 0)
    left_ids = jnp.maximum(item_table[:, 1], 0)
    right_ids = jnp.maximum(item_table[:, 2], 0)
    direct_code = (partner_ids * block_count + left_ids) * block_count + right_ids
    swapped_code = (partner_ids * block_count + right_ids) * block_count + left_ids
    direct_tiles = jnp.take(tiles, direct_code, axis=0)
    swapped_tiles = jnp.take(tiles, swapped_code, axis=0)
    tile_stack = jnp.stack([direct_tiles, swapped_tiles], axis=1)
    reduced = summed_rows(tile_stack, AUX, 0)
    aux_width = lax.axis_size(AUX)
    per_device = slot_total // aux_width
    share_start = lax.axis_index(AUX) * per_device
    my_items = lax.dynamic_slice_in_dim(item_table, share_start, per_device, 0)
    my_live = lax.dynamic_slice_in_dim(live_slots, share_start, per_device, 0)
    block_ids = jnp.arange(block_count, dtype=jnp.int32)
    virtual_blocks = vir_energies.reshape(block_count, VB)
    picks_left = (my_items[:, 1][:, None] == block_ids[None, :]).astype(jnp.float32)
    picks_right = (my_items[:, 2][:, None] == block_ids[None, :]).astype(jnp.float32)
    left_energy = jnp.dot(picks_left, virtual_blocks, precision=lax.Precision.HIGHEST)
    right_energy = jnp.dot(picks_right, virtual_blocks, precision=lax.Precision.HIGHEST)
    orbital_ids = jnp.arange(all_occ.shape[0], dtype=jnp.int32)
    partner_energy = jnp.sum(
        jnp.where(my_items[:, 0][:, None] == orbital_ids[None, :], all_occ[None, :], 0.0), axis=1
    )
    denominator = (
        left_energy[:, :, None]
        + right_energy[:, None, :]
        - occ_energies[0]
        - partner_energy[:, None, None]
    )
    direct = reduced[:, 0]
    swapped_back = jnp.transpose(reduced[:, 1], (0, 2, 1))
    energy = -jnp.sum(direct * (2.0 * direct - swapped_back) / denominator, axis=(1, 2))
    energy = jnp.where(my_live, energy, jnp.zeros_like(energy))
    total_energy = by_axis(jnp.sum(energy), OCC_AUX)
    return (energy[None, :], total_energy)


def solution(mesh):
    finer = Mesh(mesh.devices.reshape(4, 4, 2, 4, 2), ("occ_0", "occ_1", "occ_2", "aux_0", "aux_1"))
    placed = (P(OCC, None, AUX), P(OCC), P(), P(OCC, None, None), P(OCC))
    return jax.shard_map(
        local, mesh=finer, in_specs=placed, out_specs=(P(OCC, AUX), P()), check_vma=False
    )
```

profile of v0, /device:TPU:32, one launch (start us, length us, event | category | flops | bytes accessed | tf_op | source)
XLA Modules:
  0.0 493.4 jit_solution(6576529788671518339)
XLA Ops:
  7.2 0.7 all-gather.2.cloned.1.call-update
  8.0 0.7 copy.26
  8.7 145.7 %all-gather.2.cloned.1.call-done = bf16[32,256,1536]{2,1,0:T(8,128)(2,1)} async-done(((bf16[1,256,1536]{2,1,0:T(8,128)(2,1)}), bf16[32,256,1536]{2,1,0:T(8,128)(2,1)}) %all-gather.2.cloned.1.call-update) | async-done | bytes 25165840 | tf_op jit(solution)/shard_map/all_gather | solution.py:57
  154.4 13.8 %convolution_bitcast_fusion = f32[32,256,256]{2,1,0:T(8,128)} fusion(bf16[32,256,1536]{2,1,0:T(8,128)(2,1)} %all-gather.2.cloned.1.call-done, bf16[1,256,1536]{2,1,0:T(8,128)(2,1)} %param.7), kind=kOutput, calls=%fused_computation.3 | convolution fusion | flops 6442450944 | bytes 34340864 | tf_op jit(solution)/shard_map/dot_general | solution.py:55
  168.2 10.8 %reshape.37 = f32[32,2,128,2,128]{4,3,2,1,0:T(2,128)} reshape(f32[32,256,256]{2,1,0:T(8,128)} %convolution_bitcast_fusion) | data formatting | bytes 16777216 | tf_op jit(solution)/shard_map/reshape | solution.py:62
  178.9 7.8 %copy.14 = f32[32,2,128,2,128]{4,2,3,1,0:T(8,128)} copy(f32[32,2,128,2,128]{4,3,2,1,0:T(2,128)} %reshape.37) | data formatting | bytes 16777216 | tf_op jit(solution)/shard_map/reshape | solution.py:62
  186.7 4.1 gather_fusion.1
  190.8 5.8 %gather_fusion = f32[48,128,128]{2,1,0:T(8,128)} fusion(f32[128,128,128]{2,1,0:T(8,128)} %bitcast.102, s32[1024]{0:T(1024)S(1)} %pad_clamp_fusion.1), kind=kCustom, calls=%fused_computation.clone | custom fusion | bytes 6291648 | tf_op jit(solution)/shard_map/jit(_take)/gather | solution.py:71
  196.6 2.4 select_bitcast_fusion
  199.0 3.4 pad_maximum_fusion
  204.3 131.1 %all-reduce.5.cloned.1.call-done = f32[48,2,128,128]{3,2,0,1:T(8,128)} async-done(((f32[48,2,128,128]{3,2,0,1:T(8,128)}), f32[48,2,128,128]{3,2,0,1:T(8,128)}) %all-reduce.5.cloned.1.call-update) | async-done | bytes 6291472
  335.4 2.7 constant_dynamic-slice_fusion.1
  338.7 0.6 broadcast_in_dim.38
  339.4 7.9 %all-to-all-start = ((f32[32,1,1]{2,1,0:T(1,128)}), f32[32,1,1]{2,1,0:T(1,128)S(1)}, u32[]{:S(2)}, u32[]{:S(2)}) async-start(f32[32,1,1]{2,1,0:T(1,128)} %broadcast_in_dim.38), calls=%async_computation | async-start | bytes 32768 | tf_op jit(solution)/shard_map/all_to_all | solution.py:21
  349.6 4.1 all-to-all-done
  354.2 83.9 %all-reduce.7.cloned.1.call-done = f32[12,2,128,128]{3,2,0,1:T(8,128)} async-done(((f32[12,2,128,128]{3,2,0,1:T(8,128)}), f32[12,2,128,128]{3,2,0,1:T(8,128)}) %all-reduce.7.cloned.1.call-update) | async-done | bytes 1572880
  438.1 1.0 constant_dynamic-slice_fusion
  439.3 1.3 fusion.4
  440.6 1.2 fusion.14
  441.7 11.0 %psum.35 = f32[]{:T(128)} all-reduce(f32[]{:T(128)} %get-tuple-element.3), channel_id=1, replica_groups=mesh['occ_0'=4,'occ_1'=4,'occ_2'=2,'aux_0'=4,'aux_1'=2] {'occ_0'}, use_global_device_ids=true, to_apply=%region_5.7 | all-reduce | flops 1 | bytes 8 | tf_op jit(solution)/shard_map/psum | solution.py:38
  452.8 10.4 %psum.36 = f32[]{:T(128)} all-reduce(f32[]{:T(128)} %psum.35), channel_id=1, replica_groups=mesh['occ_0'=4,'occ_1'=4,'occ_2'=2,'aux_0'=4,'aux_1'=2] {'occ_1'}, use_global_device_ids=true, to_apply=%region_6.8 | all-reduce | flops 1 | bytes 8 | tf_op jit(solution)/shard_map/psum | solution.py:38
  463.2 3.1 psum.37
  466.3 11.1 %psum.38 = f32[]{:T(128)} all-reduce(f32[]{:T(128)} %psum.37), channel_id=1, replica_groups=mesh['occ_0'=4,'occ_1'=4,'occ_2'=2,'aux_0'=4,'aux_1'=2] {'aux_0'}, use_global_device_ids=true, to_apply=%region_8.10 | all-reduce | flops 1 | bytes 8 | tf_op jit(solution)/shard_map/psum | solution.py:38
  477.4 9.4 %psum.39 = f32[]{:T(128)} all-reduce(f32[]{:T(128)} %psum.38), channel_id=1, replica_groups=mesh['occ_0'=4,'occ_1'=4,'occ_2'=2,'aux_0'=4,'aux_1'=2] {'aux_1'}, use_global_device_ids=true, to_apply=%region_9.11 | all-reduce | flops 1 | bytes 8 | tf_op jit(solution)/shard_map/psum | solution.py:38
  (27 shorter events, 3.1 us)
Async XLA Ops:
  7.2 341.4 %copy-start = (f32[256]{0:T(256)S(1)}, f32[256]{0:T(256)}, u32[]{:S(2)}) copy-start(f32[256]{0:T(256)} %param.9) | copy-start | bytes 3076
  7.2 147.2 %all-gather.2.cloned.1.call-start = ((), (), s32[]{:S(2)}) async-start(), calls=%async_computation.1 | async-start | bytes 25952256 | tf_op jit(solution)/shard_map/all_gather | solution.py:57
  7.9 327.5 %all-reduce.5.cloned.1.call-start = ((), (), s32[]{:S(2)}) async-start(), calls=%async_computation.2 | async-start | bytes 12582912
  202.4 0.7 copy-start.3
  202.4 144.8 %copy-start.2 = (u32[256]{0:T(256)S(1)}, u32[256]{0:T(256)}, u32[]{:S(2)}) copy-start(u32[256]{0:T(256)} %constant.44) | copy-start | bytes 3076
  202.4 145.4 %copy-start.1 = (s32[1,48,3]{1,0,2:T(1,128)S(1)}, s32[1,48,3]{1,0,2:T(1,128)}, u32[]{:S(2)}) copy-start(s32[1,48,3]{1,0,2:T(1,128)} %param.10) | copy-start | bytes 1732
  202.4 235.6 %all-reduce.7.cloned.1.call-start = ((), (), s32[]{:S(2)}) async-start(), calls=%async_computation.3 | async-start | bytes 3145728
  339.4 14.3 %all-to-all-start = ((f32[32,1,1]{2,1,0:T(1,128)}), f32[32,1,1]{2,1,0:T(1,128)S(1)}, u32[]{:S(2)}, u32[]{:S(2)}) async-start(f32[32,1,1]{2,1,0:T(1,128)} %broadcast_in_dim.38), calls=%async_computation | async-start | bytes 32768 | tf_op jit(solution)/shard_map/all_to_all | solution.py:21
Sparse Core Ops, SparseCore 0:
  9.8 144.4 all-gather.1
  202.5 132.7 all-reduce.4
  338.2 99.8 all-reduce.6
where the time goes:
time: 494 us; the launch traced here: 493 us
  waiting for transfers between devices  365 us (74%)
  blocking collectives  45.1 us (9%)
  local copies, waits for them, and re-layouts  35.5 us (7%)
  between operations  16.5 us (3%)
  matrix products  14.1 us (3%)
  other arithmetic  8.77 us (2%)
  starting transfers between devices  7.97 us (2%)
    unnamed x5, waiting for transfers between devices  216 us
    all_gather x1, waiting for transfers between devices, local(): lax.all_gather(b_factors, OCC, axis=0, tiled=True)  146 us
    psum x5, blocking collectives, by_axis(): array = lax.psum(array, axis)  45.1 us
    reshape x2, local copies, waits for them, and re-layouts, local(): tiles = block.reshape(orbital_total, block_count, VB, block_count, VB)  18.5 us
    dot_general x1, matrix products, local(): lax.dot_general(home_panel, lax.all_gather(b_factors, OCC, axis=0, tiled=...  13.8 us
  transfers between devices with their start and end apart: 4, of which 4 were waited for; matrix products, arithmetic and copies ran while one was open for 1% of the time, Pallas kernels for 0%

commit v1 on v0

--- a/solution.py
+++ b/solution.py
@@ -54,7 +54,9 @@
     contract = (((1,), (2,)), ((), ()))
     block = lax.dot_general(
         home_panel,
-        lax.all_gather(b_factors, OCC, axis=0, tiled=True),
+        jnp.concatenate(
+            lax.all_to_all(jnp.stack([b_factors] * lax.axis_size(OCC)), OCC, 0, 0), axis=0
+        ),
         contract,
         preferred_element_type=jnp.float32,
     )

time: 494 us -> 908 us (1.84)
  waiting for transfers between devices: 365 us -> 761 us
    all_to_all x0 -> x1, waiting for transfers between devices: none -> 540 us  [local(): lax.all_to_all(jnp.stack([b_factors] * lax.axis_size(OCC)), OCC, 0, 0)]
    all_gather x1 -> x0, waiting for transfers between devices: 146 us -> none  [local(): lax.all_gather(b_factors, OCC, axis=0, tiled=True)]
    another operation x0 -> x1, local copies, waits for them, and re-layouts: none -> 9.54 us  [local(): jnp.stack([b_factors] * lax.axis_size(OCC))]
    unnamed x5 -> x4, waiting for transfers between devices: 216 us -> 218 us
  transfers between devices with their start and end apart: 4 -> 4, of which waited for: 4 -> 4; matrix products, arithmetic and copies ran while one was open for 1% -> 0% of each run, Pallas kernels for 0% -> 0%
where the time goes in v1:
time: 908 us; the launch traced here: 907 us
  waiting for transfers between devices  761 us (84%)
  blocking collectives  45.1 us (5%)
  local copies, waits for them, and re-layouts  44.3 us (5%)
  between operations  16.8 us (2%)
  starting transfers between devices  16.7 us (2%)
  matrix products  13.9 us (2%)
    all_to_all x1, waiting for transfers between devices, local(): lax.all_to_all(jnp.stack([b_factors] * lax.axis_size(OCC)), OCC, 0, 0)  540 us
    unnamed x4, waiting for transfers between devices  218 us
    psum x5, blocking collectives, by_axis(): array = lax.psum(array, axis)  45.1 us
    reshape x2, local copies, waits for them, and re-layouts, local(): tiles = block.reshape(orbital_total, block_count, VB, block_count, VB)  18.5 us
  transfers between devices with their start and end apart: 4, of which 4 were waited for; matrix products, arithmetic and copies ran while one was open for 0% of the time, Pallas kernels for 0%

profile of v1, /device:TPU:32, one launch (start us, length us, event | category | flops | bytes accessed | tf_op | source)
XLA Modules:
  0.0 907.1 jit_solution(14793306959161622840)
XLA Ops:
  7.2 9.5 %stack.8 = bf16[32,1,256,1536]{3,2,1,0:T(8,128)(2,1)} broadcast(bf16[256,1536]{1,0:T(8,128)(2,1)} %bitcast.107), dimensions={2,3} | broadcast | bytes 25952256 | tf_op jit(solution)/shard_map/stack | solution.py:58
  16.7 8.8 all-to-all-start
  25.6 539.7 %all-to-all-done = bf16[32,1,256,1536]{3,2,1,0:T(8,128)(2,1)} async-done(((bf16[32,1,256,1536]{3,2,1,0:T(8,128)(2,1)}), bf16[32,1,256,1536]{3,2,1,0:T(8,128)(2,1)}, u32[]{:S(2)}, u32[]{:S(2)}) %all-to-all-start) | async-done | bytes 25165856 | tf_op jit(solution)/shard_map/all_to_all | solution.py:58
  565.4 13.6 %fusion.2 = f32[32,256,256]{2,1,0:T(8,128)} fusion(bf16[32,1,256,1536]{3,2,1,0:T(8,128)(2,1)} %all-to-all-done, bf16[1,256,1536]{2,1,0:T(8,128)(2,1)S(1)} %copy-done.1), kind=kOutput, calls=%fused_computation.5 | convolution fusion | flops 6442450944 | bytes 34340864 | tf_op jit(solution)/shard_map/dot_general | solution.py:55
  578.9 10.8 %reshape.44 = f32[32,2,128,2,128]{4,3,2,1,0:T(2,128)} reshape(f32[32,256,256]{2,1,0:T(8,128)} %fusion.2) | data formatting | bytes 16777216 | tf_op jit(solution)/shard_map/reshape | solution.py:64
  589.7 7.8 copy.14
  597.4 4.1 gather_fusion.1
  601.6 5.8 gather_fusion
  607.4 2.4 select_bitcast_fusion
  609.8 3.4 pad_maximum_fusion
  615.1 133.7 %all-reduce.5.cloned.1.call-done = f32[48,2,128,128]{3,2,0,1:T(8,128)} async-done(((f32[48,2,128,128]{3,2,0,1:T(8,128)}), f32[48,2,128,128]{3,2,0,1:T(8,128)}) %all-reduce.5.cloned.1.call-update) | async-done | bytes 6291472
  748.8 2.7 constant_dynamic-slice_fusion.1
  752.2 0.6 broadcast_in_dim.38
  752.8 7.9 all-to-all-start.1
  763.1 4.1 all-to-all-done.1
  767.6 83.9 %all-reduce.7.cloned.1.call-done = f32[12,2,128,128]{3,2,0,1:T(8,128)} async-done(((f32[12,2,128,128]{3,2,0,1:T(8,128)}), f32[12,2,128,128]{3,2,0,1:T(8,128)}) %all-reduce.7.cloned.1.call-update) | async-done | bytes 1572880
  851.5 1.0 constant_dynamic-slice_fusion
  852.7 1.3 fusion.9
  854.0 1.2 fusion.19
  855.2 11.0 %psum.35 = f32[]{:T(128)} all-reduce(f32[]{:T(128)} %get-tuple-element.3), channel_id=1, replica_groups=mesh['occ_0'=4,'occ_1'=4,'occ_2'=2,'aux_0'=4,'aux_1'=2] {'occ_0'}, use_global_device_ids=true, to_apply=%region_5.7 | all-reduce | flops 1 | bytes 8 | tf_op jit(solution)/shard_map/psum | solution.py:38
  866.2 10.4 %psum.36 = f32[]{:T(128)} all-reduce(f32[]{:T(128)} %psum.35), channel_id=1, replica_groups=mesh['occ_0'=4,'occ_1'=4,'occ_2'=2,'aux_0'=4,'aux_1'=2] {'occ_1'}, use_global_device_ids=true, to_apply=%region_6.8 | all-reduce | flops 1 | bytes 8 | tf_op jit(solution)/shard_map/psum | solution.py:38
  876.6 3.1 psum.37
  879.7 11.1 %psum.38 = f32[]{:T(128)} all-reduce(f32[]{:T(128)} %psum.37), channel_id=1, replica_groups=mesh['occ_0'=4,'occ_1'=4,'occ_2'=2,'aux_0'=4,'aux_1'=2] {'aux_0'}, use_global_device_ids=true, to_apply=%region_8.10 | all-reduce | flops 1 | bytes 8 | tf_op jit(solution)/shard_map/psum | solution.py:38
  890.8 9.4 %psum.39 = f32[]{:T(128)} all-reduce(f32[]{:T(128)} %psum.38), channel_id=1, replica_groups=mesh['occ_0'=4,'occ_1'=4,'occ_2'=2,'aux_0'=4,'aux_1'=2] {'aux_1'}, use_global_device_ids=true, to_apply=%region_9.11 | all-reduce | flops 1 | bytes 8 | tf_op jit(solution)/shard_map/psum | solution.py:38
  (29 shorter events, 3.0 us)
Async XLA Ops:
  7.2 754.8 %copy-start = (f32[256]{0:T(256)S(1)}, f32[256]{0:T(256)}, u32[]{:S(2)}) copy-start(f32[256]{0:T(256)} %param.9) | copy-start | bytes 3076
  16.7 8.9 copy-start.2
  16.7 548.6 %copy-start.1 = (bf16[1,256,1536]{2,1,0:T(8,128)(2,1)S(1)}, bf16[1,256,1536]{2,1,0:T(8,128)(2,1)}, u32[]{:S(2)}) copy-start(bf16[1,256,1536]{2,1,0:T(8,128)(2,1)} %param.7) | copy-start | bytes 2359300
  16.7 548.6 %all-to-all-start = ((bf16[32,1,256,1536]{3,2,1,0:T(8,128)(2,1)}), bf16[32,1,256,1536]{3,2,1,0:T(8,128)(2,1)}, u32[]{:S(2)}, u32[]{:S(2)}) async-start(bf16[32,1,256,1536]{3,2,1,0:T(8,128)(2,1)} %stack.8), calls=%async_computation | async-start | bytes 50331648 | tf_op jit(solution)/shard_map/all_to_all | solution.py:58
  25.5 723.3 %all-reduce.5.cloned.1.call-start = ((), (), s32[]{:S(2)}) async-start(), calls=%async_computation.2 | async-start | bytes 12582912
  613.1 0.7 copy-start.4
  613.2 147.5 %copy-start.3 = (u32[256]{0:T(256)S(1)}, u32[256]{0:T(256)}, u32[]{:S(2)}) copy-start(u32[256]{0:T(256)} %constant.44) | copy-start | bytes 3076
  613.2 238.3 %all-reduce.7.cloned.1.call-start = ((), (), s32[]{:S(2)}) async-start(), calls=%async_computation.3 | async-start | bytes 3145728
  752.8 14.3 %all-to-all-start.1 = ((f32[32,1,1]{2,1,0:T(1,128)}), f32[32,1,1]{2,1,0:T(1,128)S(1)}, u32[]{:S(2)}, u32[]{:S(2)}) async-start(f32[32,1,1]{2,1,0:T(1,128)} %broadcast_in_dim.38), calls=%async_computation.1 | async-start | bytes 32768 | tf_op jit(solution)/shard_map/all_to_all | solution.py:21
Sparse Core Ops, SparseCore 0:
  613.3 135.4 all-reduce.4
  751.6 99.8 all-reduce.6
